TPU v7x, 32 devices: a whole 2x2x4 slice. The times are simulated.
32 devices in a mesh: group: 4 (over z), shard: 8 (over y, x, core).
Axes of the slice: x: 2, y: 2, z: 4, core: 2. Of those that a mesh axis runs over, the one named last changes fastest.
Arguments:
- hidden_state: bfloat16 [512, 8192], P('group', 'shard'), may hold values from -40 to 40
- attn_gain: bfloat16 [8192], replicated, may hold values from 0.5 to 1.5
- ffn_gain: bfloat16 [8192], replicated, may hold values from 0.5 to 1.5
- w_query: bfloat16 [8192, 8192], P('group', 'shard'), may hold values from -0.125 to 0.125
- w_keyval: bfloat16 [8192, 2048], P('group', 'shard'), may hold values from -0.0625 to 0.0625
- w_output: bfloat16 [8192, 8192], P('shard', 'group'), may hold values from -0.0625 to 0.0625
- cache_keys: bfloat16 [512, 8, 192, 128], P(('group', 'shard')), may hold values from -256 to 256
- cache_values: bfloat16 [512, 8, 192, 128], P(('group', 'shard')), may hold values from -6 to 6
- lengths: int32 [512], P('group'), may hold values from 2 to 192, as said below
Outputs:
- branch: bfloat16 [512, 8192], P('group', 'shard')
- ffn_input: bfloat16 [512, 8192], P('group', 'shard')
Inputs may be any that keep to these rules, and one draw needn't show every extreme that they name: `lengths`: in every aligned block of 16 sequences, at least one has all 192 cached positions live.
All inputs are finite; a program needn't handle non-finite values.
Results may differ from a plain program's by a relative error of at most 0.012.
The roundings to bfloat16 on the way count: a program that leaves them out, or rounds other values in their place, can miss the bound.
Values may be sent and summed in bfloat16 or wider, within the bound.
A program may use at most 128 MiB of HBM per device.

v0:
```python
import functools

import jax
import jax.numpy as jnp
from jax import lax
from jax.experimental import pallas as pl
from jax.experimental.pallas import tpu as pltpu
from jax.sharding import PartitionSpec as P

epsilon = 1e-05
rope_base = 500000.0
MESH = pl.DeviceIdType.MESH
VMEM = pl.BlockSpec(memory_space=pltpu.VMEM)
BF = jnp.bfloat16
F32 = jnp.float32


def device(group, shard):
    return {"group": group, "shard": shard}


def partner_of(k, sizes, sign=1):
    groups, shards = sizes
    g, s = lax.axis_index("group"), lax.axis_index("shard")
    dg, ds = k // shards, k % shards
    if sign > 0:
        return lax.rem(g + dg, groups), lax.rem(s + ds, shards)
    return lax.rem(g - dg + groups, groups), lax.rem(s - ds + shards, shards)


def greet(sizes, total):
    barrier = pltpu.get_barrier_semaphore()

    def signal(k, carry):
        pl.semaphore_signal(
            barrier, inc=1, device_id=device(*partner_of(k, sizes)), device_id_type=MESH
        )
        return carry

    lax.fori_loop(1, total, signal, 0)
    pl.semaphore_wait(barrier, total - 1)


def remote(src, dst, send, recv, where):
    return pltpu.make_async_remote_copy(
        src_ref=src,
        dst_ref=dst,
        send_sem=send,
        recv_sem=recv,
        device_id=device(*where),
        device_id_type=MESH,
    )


def exchange_kernel(sizes, total, src_at, dst_at, count, *refs):
    ins, outs = refs[:count], refs[count : 2 * count]
    sends, recvs, own = refs[2 * count :]
    g, s = lax.axis_index("group"), lax.axis_index("shard")
    locals_ = [
        pltpu.make_async_copy(src_at(a, g, s), dst_at(b, g, s), own.at[i])
        for i, (a, b) in enumerate(zip(ins, outs))
    ]
    for c in locals_:
        c.start()
    greet(sizes, total)

    def start(j, carry):
        k = lax.rem(j, sizes[0]) * sizes[1] + j // sizes[0]
        pg, ps = partner_of(k, sizes)
        for i in range(count):
            remote(
                src_at(ins[i], pg, ps),
                dst_at(outs[i], g, s),
                sends.at[i, k],
                recvs.at[i, k],
                (pg, ps),
            ).start()
        return carry

    lax.fori_loop(1, total, start, 0)

    def finish(j, carry):
        k = lax.rem(j, sizes[0]) * sizes[1] + j // sizes[0]
        pg, ps = partner_of(k, sizes)
        fg, fs = partner_of(k, sizes, -1)
        for i in range(count):
            copy = remote(
                src_at(ins[i], pg, ps),
                dst_at(outs[i], fg, fs),
                sends.at[i, k],
                recvs.at[i, k],
                (pg, ps),
            )
            copy.wait_send()
            copy.wait_recv()
        return carry

    lax.fori_loop(1, total, finish, 0)
    for c in locals_:
        c.wait()


def exchange(arrays, outs, sizes, total, src_at, dst_at, ident):
    count = len(arrays)
    return pl.pallas_call(
        functools.partial(exchange_kernel, sizes, total, src_at, dst_at, count),
        out_shape=[jax.ShapeDtypeStruct(o, a.dtype) for o, a in zip(outs, arrays)],
        in_specs=[VMEM] * count,
        out_specs=[VMEM] * count,
        scratch_shapes=[
            pltpu.SemaphoreType.DMA((count, total)),
            pltpu.SemaphoreType.DMA((count, total)),
            pltpu.SemaphoreType.DMA((count,)),
        ],
        compiler_params=pltpu.CompilerParams(collective_id=ident, has_side_effects=True),
    )(*arrays)


def spread_kernel(
    sizes, x_ref, ss_ref, all_ref, sums_ref, held, s0, r0, s1, r1, s2, r2, sa, ra, sb, rb, own
):
    groups, shards = sizes
    chips = shards // 2
    ratio = shards // groups
    rows = x_ref.shape[0] // shards
    width = x_ref.shape[1]
    g, s = lax.axis_index("group"), lax.axis_index("shard")
    chip, core = s // 2, lax.rem(s, 2)
    sibling = chip * 2 + 1 - core
    keep = pltpu.make_async_copy(ss_ref, sums_ref.at[g, s], own.at[0])
    keep.start()
    greet(sizes, groups * shards)
    to_group, piece = s // ratio, lax.rem(s, ratio)

    def hop(ds):
        t = lax.rem(s + ds, shards)
        src = x_ref.at[pl.ds(pl.multiple_of(t * rows, rows), rows), :]
        dst = held.at[g, :, pl.ds(pl.multiple_of(piece * width, width), width)]
        return src, dst, (to_group, t)

    slot = g * ratio + piece
    for ds in range(1, shards):
        src, dst, where = hop(ds)
        remote(src, dst, s0.at[ds], r0.at[slot], where).start()
    src, dst, where = hop(0)

    @pl.when(to_group != g)
    def _():
        remote(src, dst, s0.at[0], r0.at[slot], where).start()

    @pl.when(to_group == g)
    def _():
        pltpu.make_async_copy(src, dst, r0.at[slot]).start()

    def plane_sum(ds, sent):
        to, back = lax.rem(s + ds, shards), lax.rem(s - ds + shards, shards)
        slot = s if sent else back
        return remote(ss_ref, sums_ref.at[g, slot], s1.at[ds], r1.at[ds], (g, to))

    def group_sum(dg, sent):
        to, back = lax.rem(g + dg, groups), lax.rem(g - dg + groups, groups)
        slot = g if sent else back
        return remote(sums_ref.at[g], sums_ref.at[slot], s2.at[dg], r2.at[dg], (to, s))

    for ds in range(1, shards):
        plane_sum(ds, True).start()

    order = sorted(range(groups), key=lambda d: min(d, groups - d))

    def came(dg):
        return lax.rem(g - dg + groups, groups)

    def ring(dg, c):
        to = lax.rem(chip + c, chips) * 2 + core
        return remote(
            held.at[came(dg)], all_ref.at[s, came(dg)], sa.at[dg, c], ra.at[dg, c], (g, to)
        )

    def pair(dg, c):
        if c == 0:
            src, dst = held.at[came(dg)], all_ref.at[s, came(dg)]
        else:
            u = lax.rem(chip + chips - c, chips) * 2 + core
            src = dst = all_ref.at[u, came(dg)]
        return remote(src, dst, sb.at[dg, c], rb.at[dg, c], (g, sibling))

    def ring_slot(dg, c, which):
        u = lax.rem(chip + chips - c, chips) * 2 + which
        return all_ref.at[u, came(dg)]

    def forward(dg):
        for c in range(1, chips):
            dst = ring_slot(dg, c, core)
            remote(dst, dst, sa.at[dg, c], ra.at[dg, c], (g, sibling)).wait_recv()
            pair(dg, c).start()

    def mine(dg):
        return pltpu.make_async_copy(
            held.at[came(dg)], all_ref.at[s, came(dg)], own.at[1 + dg]
        )

    for i, dg in enumerate(order):
        for h in range(ratio):
            dst = held.at[came(dg), :, pl.ds(h * width, width)]
            pltpu.make_async_copy(dst, dst, r0.at[came(dg) * ratio + h]).wait()
        for c in range(1, chips):
            ring(dg, c).start()
        pair(dg, 0).start()
        mine(dg).start()
        if i == 0:
            keep.wait()
            for ds in range(1, shards):
                plane_sum(ds, False).wait_recv()
            for d in range(1, groups):
                group_sum(d, True).start()
        else:
            forward(order[i - 1])
    forward(order[-1])
    for dg in order:
        for c in range(chips):
            dst = ring_slot(dg, c, 1 - core)
            remote(dst, dst, sb.at[dg, c], rb.at[dg, c], (g, sibling)).wait_recv()
    for dg in order:
        for c in range(chips):
            if c:
                ring(dg, c).wait_send()
            pair(dg, c).wait_send()
        mine(dg).wait()
    for ds in range(1, shards):
        src, dst, where = hop(ds)
        remote(src, dst, s0.at[ds], r0.at[slot], where).wait_send()
        plane_sum(ds, True).wait_send()
    src, dst, where = hop(0)

    @pl.when(to_group != g)
    def _():
        remote(src, dst, s0.at[0], r0.at[slot], where).wait_send()

    for d in range(1, groups):
        group_sum(d, True).wait_send()
        group_sum(d, False).wait_recv()


def spread(x, ss, sizes):
    groups, shards = sizes
    ratio = shards // groups
    rows = x.shape[0] // shards
    wide = x.shape[1] * ratio
    dma = pltpu.SemaphoreType.DMA
    return pl.pallas_call(
        functools.partial(spread_kernel, sizes),
        out_shape=[
            jax.ShapeDtypeStruct((shards, groups, rows, wide), x.dtype),
            jax.ShapeDtypeStruct((groups, shards) + ss.shape, ss.dtype),
        ],
        in_specs=[VMEM] * 2,
        out_specs=[VMEM] * 2,
        scratch_shapes=[
            pltpu.VMEM((groups, rows, wide), x.dtype),
            dma((shards,)),
            dma((shards,)),
            dma((shards,)),
            dma((shards,)),
            dma((groups,)),
            dma((groups,)),
            dma((groups, shards // 2)),
            dma((groups, shards // 2)),
            dma((groups, shards // 2)),
            dma((groups, shards // 2)),
            dma((1 + groups,)),
        ],
        compiler_params=pltpu.CompilerParams(collective_id=1, has_side_effects=True),
    )(x, ss)


pieces = 4
lanes = 128


def finish_kernel(
    sizes,
    p_ref,
    x_ref,
    gain_ref,
    branch_ref,
    ffn_ref,
    sib,
    mid,
    got,
    total_ref,
    fin,
    squares,
    s0,
    r0,
    s1,
    r1,
    s2,
    r2,
    s3,
    r3,
):
    groups, shards = sizes
    chips = shards // 2
    tokens, width = x_ref.shape
    model = width * shards
    g, s = lax.axis_index("group"), lax.axis_index("shard")
    chip, core = s // 2, lax.rem(s, 2)
    sibling = chip * 2 + 1 - core
    greet(sizes, groups * shards)
    order = list(range(1, chips)) + [0]
    span = tokens // pieces

    def block(c):
        return lax.rem(chip + c, chips)

    def half(which):
        return pl.ds(pl.multiple_of(which * width, width), width)

    def rows(q):
        return pl.ds(q * span, span)

    def near(q, c):
        a = block(c)
        return remote(
            p_ref.at[a, rows(q), half(1 - core)],
            sib.at[a, rows(q)],
            s0.at[q, c],
            r0.at[q, c],
            (g, sibling),
        )

    def far(q, c):
        a = block(c)
        return remote(
            mid.at[a, rows(q)],
            got.at[c, rows(q)],
            s1.at[q, c],
            r1.at[q, c],
            (g, a * 2 + core),
        )

    def swap(q):
        return remote(
            total_ref.at[rows(q)], fin.at[rows(q)], s2.at[q], r2.at[q], (chip, g * 2 + core)
        )

    for q in range(pieces):
        for c in order:
            near(q, c).start()
    for q in range(pieces):
        for c in order:
            a = block(c)
            near(q, c).wait_recv()
            mid[a, rows(q)] = (
                p_ref[a, rows(q), half(core)].astype(F32) + sib[a, rows(q)].astype(F32)
            ).astype(BF)
            if c:
                far(q, c).start()
    for q in range(pieces):
        acc = mid[chip, rows(q)].astype(F32)
        for c in order[:-1]:
            far(q, c).wait_recv()
            acc = acc + got[c, rows(q)].astype(F32)
        total_ref[rows(q)] = acc.astype(BF)

        @pl.when(chip != g)
        def _():
            swap(q).start()

        @pl.when(chip == g)
        def _():
            pltpu.make_async_copy(total_ref.at[rows(q)], fin.at[rows(q)], r2.at[q]).start()

    parts = []
    for q in range(pieces):
        pltpu.make_async_copy(fin.at[rows(q)], fin.at[rows(q)], r2.at[q]).wait()
        branch_ref[rows(q)] = fin[rows(q)]
        part = jnp.zeros((span, lanes), F32)
        for j in range(width // lanes):
            cols = pl.ds(j * lanes, lanes)
            stream = x_ref[rows(q), cols].astype(F32) + fin[rows(q), cols].astype(F32)
            part = part + stream * stream
        parts.append(part)
    flipped = jnp.concatenate(parts, axis=0).T
    squares[s] = jnp.sum(flipped, axis=0, keepdims=True)

    def tell(ds, slot):
        to = lax.rem(s + ds, shards)
        return remote(squares.at[slot], squares.at[slot], s3.at[ds], r3.at[ds], (g, to))

    for ds in range(1, shards):
        tell(ds, s).start()
    for q in range(pieces):
        for c in order:
            near(q, c).wait_send()
            if c:
                far(q, c).wait_send()

        @pl.when(chip != g)
        def _():
            swap(q).wait_send()

    for ds in range(1, shards):
        tell(ds, lax.rem(s - ds + shards, shards)).wait_recv()
    square_sum = squares[0]
    for t in range(1, shards):
        square_sum = square_sum + squares[t]
    inverse = lax.rsqrt(square_sum / model + epsilon)
    inverse = jnp.broadcast_to(inverse, (lanes, tokens)).T
    for j in range(width // lanes):
        cols = pl.ds(j * lanes, lanes)
        stream = x_ref[:, cols].astype(F32) + fin[:, cols].astype(F32)
        ffn_ref[:, cols] = (stream * inverse * gain_ref[:, cols]).astype(BF)
    for ds in range(1, shards):
        tell(ds, s).wait_send()


def finish(partial, x, gain, sizes):
    groups, shards = sizes
    chips = shards // 2
    tokens, width = x.shape
    dma = pltpu.SemaphoreType.DMA
    return pl.pallas_call(
        functools.partial(finish_kernel, sizes),
        out_shape=[jax.ShapeDtypeStruct((tokens, width), BF)] * 2,
        in_specs=[VMEM] * 3,
        out_specs=[VMEM] * 2,
        scratch_shapes=[
            pltpu.VMEM((chips, tokens, width), BF),
            pltpu.VMEM((chips, tokens, width), BF),
            pltpu.VMEM((chips, tokens, width), BF),
            pltpu.VMEM((tokens, width), BF),
            pltpu.VMEM((tokens, width), BF),
            pltpu.VMEM((shards, 1, tokens), F32),
            dma((pieces, chips)),
            dma((pieces, chips)),
            dma((pieces, chips)),
            dma((pieces, chips)),
            dma((pieces,)),
            dma((pieces,)),
            dma((shards,)),
            dma((shards,)),
        ],
        compiler_params=pltpu.CompilerParams(collective_id=4, has_side_effects=True),
    )(partial, x, gain)


def rotate(heads_block, position):
    head_dim = heads_block.shape[-1]
    half_dim = head_dim // 2
    frequency = rope_base ** (-2.0 * jnp.arange(half_dim, dtype=jnp.float32) / head_dim)
    angles = position.astype(jnp.float32)[:, None] * frequency[None, :]
    cosine = jnp.cos(angles)[:, None, :]
    sine_part = jnp.sin(angles)[:, None, :]
    lower_half = heads_block[..., :half_dim]
    upper_half = heads_block[..., half_dim:]
    return jnp.concatenate(
        [
            lower_half * cosine - upper_half * sine_part,
            upper_half * cosine + lower_half * sine_part,
        ],
        axis=-1,
    )


def attend(grouped, new_keys, new_values, cache_keys, cache_values, lengths):
    cache_len, head_dim = cache_keys.shape[2:]
    score_scale = head_dim ** (-0.5)
    scores = (
        jnp.einsum("nkgd,nkld->nkgl", grouped, cache_keys, preferred_element_type=jnp.float32)
        * score_scale
    )
    self_score = (
        jnp.einsum("nkgd,nkd->nkg", grouped, new_keys, preferred_element_type=jnp.float32)
        * score_scale
    )
    live_mask = jnp.arange(cache_len, dtype=jnp.int32)[None, :] < lengths[:, None]
    scores = jnp.where(live_mask[:, None, None, :], scores, -1e30)
    row_top = jnp.maximum(jnp.max(scores, axis=3), self_score)
    exp_scores = jnp.exp(scores - row_top[..., None])
    self_weight = jnp.exp(self_score - row_top)
    denom_sum = jnp.sum(exp_scores, axis=3) + self_weight
    weight_bf = (exp_scores / denom_sum[..., None]).astype(jnp.bfloat16)
    self_bf = (self_weight / denom_sum).astype(jnp.bfloat16)
    context = jnp.einsum(
        "nkgl,nkld->nkgd", weight_bf, cache_values, preferred_element_type=jnp.float32
    )
    context = (
        context
        + self_bf.astype(jnp.float32)[..., None] * new_values.astype(jnp.float32)[:, :, None, :]
    )
    return context.astype(jnp.bfloat16)


def local(
    sizes,
    hidden_state,
    attn_gain,
    ffn_gain,
    w_query,
    w_keyval,
    w_output,
    cache_keys,
    cache_values,
    lengths,
):
    groups, shards = sizes
    total = groups * shards
    tokens, width = hidden_state.shape
    seqs, kv_heads, _, head_dim = cache_keys.shape
    g, s = lax.axis_index("group"), lax.axis_index("shard")
    model = width * shards
    depth = w_query.shape[0]
    q_cols, kv_cols = w_query.shape[1], w_keyval.shape[1]
    resident = hidden_state.astype(F32)

    squares = jnp.sum(resident * resident, axis=1)[None, :]
    block, sums = spread(hidden_state, squares, sizes)
    square_sum = jnp.sum(sums[:, :, 0, :], axis=1)
    inverse = lax.rsqrt(square_sum / model + epsilon)
    inverse = inverse.reshape(groups, shards, seqs).transpose(1, 0, 2)
    gain = lax.dynamic_slice_in_dim(attn_gain, g * depth, depth).astype(F32)
    normed = (block.astype(F32) * inverse[..., None] * gain).astype(BF)
    normed = normed.reshape(total * seqs, depth)
    part_q = jnp.dot(normed, w_query, preferred_element_type=F32).astype(BF)
    part_kv = jnp.dot(normed, w_keyval, preferred_element_type=F32).astype(BF)
    cols = q_cols + kv_cols
    part = jnp.concatenate([part_q, part_kv], axis=1)

    (got,) = exchange(
        [part.reshape(shards, groups, seqs, cols)],
        [(groups, shards, seqs, cols)],
        sizes,
        total,
        lambda ref, pg, ps: ref.at[ps, pg],
        lambda ref, pg, ps: ref.at[pg, ps],
        2,
    )
    owner_len = lax.dynamic_slice_in_dim(lengths, s * seqs, seqs)
    fresh = jnp.sum(got.astype(F32), axis=0).transpose(1, 0, 2)
    queries, keyval = fresh[..., :q_cols], fresh[..., q_cols:]
    heads = shards * q_cols // head_dim
    grouped = (
        rotate(queries.reshape(seqs, heads, head_dim), owner_len)
        .astype(BF)
        .reshape(seqs, kv_heads, heads // kv_heads, head_dim)
    )
    keyval = keyval.reshape(seqs, 2 * kv_heads, head_dim)
    new_keys = rotate(keyval[:, :kv_heads], owner_len).astype(BF)
    new_values = keyval[:, kv_heads:].astype(BF)
    context = attend(grouped, new_keys, new_values, cache_keys, cache_values, owner_len)
    context = context.reshape(seqs, shards, q_cols).transpose(1, 0, 2)

    (rows,) = exchange(
        [context],
        [(groups, shards, seqs, q_cols)],
        sizes,
        total,
        lambda ref, pg, ps: ref.at[ps],
        lambda ref, pg, ps: ref.at[pg, ps],
        3,
    )
    partial = jnp.dot(
        rows.reshape(total * seqs, q_cols), w_output, preferred_element_type=F32
    ).astype(BF)
    ffn_scale = lax.dynamic_slice_in_dim(ffn_gain, s * width, width).astype(F32)[None, :]
    branch, ffn_input = finish(
        partial.reshape(groups, tokens, w_output.shape[1]), hidden_state, ffn_scale, sizes
    )
    return (branch, ffn_input)


def solution(mesh):
    sizes = (mesh.shape["group"], mesh.shape["shard"])
    placed = (
        P("group", "shard"),
        P(),
        P(),
        P("group", "shard"),
        P("group", "shard"),
        P("shard", "group"),
        P(("group", "shard"), None, None, None),
        P(("group", "shard"), None, None, None),
        P("group"),
    )
    return jax.shard_map(
        functools.partial(local, sizes),
        mesh=mesh,
        in_specs=placed,
        out_specs=(P("group", "shard"), P("group", "shard")),
        check_vma=False,
    )
```

profile of v0, /device:TPU:0, one launch (start us, length us, event | category | flops | bytes accessed | tf_op | source)
XLA Modules:
  0.0 176.4 jit_solution(8059224291804141446)
XLA Ops:
  0.7 0.8 dynamic-slice_convert_fusion
  1.4 1.6 multiply_reduce_fusion
  3.0 36.8 %shard_map.104 = (bf16[8,4,16,2048]{3,2,1,0:T(8,128)(2,1)}, f32[4,8,1,128]{3,2,1,0:T(1,128)}) custom-call(bf16[128,1024]{1,0:T(8,128)(2,1)} %x_ref.3, f32[1,128]{1,0:T(1,128)} %bitcast.41), custom_call_target="tpu_custom_call" | custom-call | tf_op jit(solution)/shard_map/pallas_call | solution.py:250
  39.9 0.7 reduce_sum.37
  40.7 2.3 %multiply_convert_fusion = bf16[8,4,16,2048]{3,2,1,0:T(8,128)(2,1)S(1)} fusion(bf16[8,4,16,2048]{3,2,1,0:T(8,128)(2,1)} %get-tuple-element.4, f32[2048]{0:T(1024)S(1)} %dynamic-slice_convert_fusion, f32[8,4,16]{2,1,0:T(4,128)S(1)} %copy.19), kind=kLoop, calls=%fused_computation | loop fusion | flops 4194304 | bytes 4204544 | tf_op jit(solution)/shard_map/convert_element_type | solution.py:523
  43.0 0.5 copy-done.2
  43.5 2.3 %convolution_convert_fusion.1 = bf16[512,1024]{1,0:T(8,128)(2,1)S(1)} fusion(bf16[512,2048]{1,0:T(8,128)(2,1)S(1)} %bitcast.33, bf16[2048,1024]{1,0:T(8,128)(2,1)S(1)} %copy-done.2), kind=kOutput, calls=%fused_computation.3 | convolution fusion | flops 2148007936 | bytes 7340032 | tf_op jit(solution)/shard_map/dot_general | solution.py:525
  45.9 0.7 convolution_convert_fusion.2
  46.6 1.2 pad_maximum_fusion
  47.8 37.0 %shard_map.105 = bf16[4,8,16,1280]{3,2,1,0:T(8,128)(2,1)} custom-call(bf16[8,4,16,1280]{3,2,1,0:T(8,128)(2,1)} %bitcast.29), custom_call_target="tpu_custom_call" | custom-call | tf_op jit(solution)/shard_map/pallas_call | solution.py:105
  84.7 1.6 convert_reduce_fusion
  86.9 0.3 copy.21
  87.3 0.2 fusion.5
  87.6 0.3 fusion.7
  88.0 6.6 %fusion.15 = (f32[16,8,8]{2,1,0:T(8,128)S(1)}, f32[16,8,8,192]{3,2,1,0:T(8,128)S(1)}) fusion(bf16[16,8,192,128]{3,2,1,0:T(8,128)(2,1)} %param.15, bf16[16,8,8,64]{3,2,1,0:T(8,128)(2,1)S(1)} %get-tuple-element.9, bf16[16,8,8,64]{3,2,1,0:T(8,128)(2,1)S(1)} %get-tuple-element.8, pred[16,192]{1,0:T(8,128)(4,1)S(1)} %iota_compare_fusion), kind=kOutput, calls=%fused_computation.44 | convolution fusion | flops 51444736 | bytes 7347200 | tf_op jit(solution)/shard_map/nkgd,nkld->nkgl/dot_general | solution.py:470
  94.6 0.4 fusion.2
  95.1 1.8 %fusion.1 = bf16[16,8,8,128]{3,2,1,0:T(8,128)(2,1)S(1)} fusion(bf16[16,8,192,128]{3,2,1,0:T(8,128)(2,1)S(1)} %bitcast.43, f32[16,8,8,192]{3,2,1,0:T(8,128)S(1)} %get-tuple-element.17, f32[16,8,8]{2,1,0:T(8,128)S(1)} %get-tuple-element.11, f32[16,8,8]{2,1,0:T(8,128)S(1)} %multiply_maximum_fusion, f32[16,8,128]{2,1,0:T(8,128)S(1)} %fusion.10, ...), kind=kOutput, calls=%fused_computation.8 | convolution fusion | flops 51314688 | bytes 7417856 | tf_op jit(solution)/shard_map/nkgl,nkld->nkgd/dot_general | solution.py:485
  97.1 0.9 copy.31
  97.9 30.3 %shard_map.106 = bf16[4,8,16,1024]{3,2,1,0:T(8,128)(2,1)} custom-call(bf16[8,16,1024]{2,1,0:T(8,128)(2,1)} %bitcast.36), custom_call_target="tpu_custom_call" | custom-call | tf_op jit(solution)/shard_map/pallas_call | solution.py:105
  128.3 6.2 %convolution_convert_fusion = bf16[512,2048]{1,0:T(8,128)(2,1)} fusion(bf16[512,1024]{1,0:T(8,128)(2,1)} %bitcast.35, bf16[1024,2048]{1,0:T(8,128)(2,1)} %param.14), kind=kOutput, calls=%fused_computation.1 | convolution fusion | flops 2148532224 | bytes 7340032 | tf_op jit(solution)/shard_map/dot_general | solution.py:563
  134.5 1.3 dynamic-slice_convert_fusion.1
  135.8 37.3 %shard_map.107 = (bf16[128,1024]{1,0:T(8,128)(2,1)}, bf16[128,1024]{1,0:T(8,128)(2,1)}) custom-call(bf16[4,128,2048]{2,1,0:T(8,128)(2,1)} %bitcast.32, bf16[128,1024]{1,0:T(8,128)(2,1)} %x_ref.3, f32[1,1024]{1,0:T(1,128)} %bitcast.40), custom_call_target="tpu_custom_call" | custom-call | tf_op jit(solution)/shard_map/pallas_call | solution.py:423
  173.1 1.7 copy.34
  174.8 1.7 copy.35
  (28 shorter events, 1.0 us)
Async XLA Ops:
  0.6 45.3 %copy-start = (bf16[2048,256]{1,0:T(8,128)(2,1)S(1)}, bf16[2048,256]{1,0:T(8,128)(2,1)}, u32[]{:S(2)}) copy-start(bf16[2048,256]{1,0:T(8,128)(2,1)} %param.13) | copy-start | bytes 3145732
  40.7 2.8 %copy-start.2 = (bf16[2048,1024]{1,0:T(8,128)(2,1)S(1)}, bf16[2048,1024]{1,0:T(8,128)(2,1)}, u32[]{:S(2)}) copy-start(bf16[2048,1024]{1,0:T(8,128)(2,1)} %param.12) | copy-start | bytes 12582916
  47.8 38.7 %copy-start.1 = (s32[128]{0:T(128)S(1)}, s32[128]{0:T(128)}, u32[]{:S(2)}) copy-start(s32[128]{0:T(128)} %param.17) | copy-start | bytes 1540
  87.3 7.8 %slice-start = ((s8[6291456]{0:T(1024)(128)(4,1)}), s8[4194304]{0:T(1024)(128)(4,1)S(1)}, s32[]{:S(2)}) async-start(s8[6291456]{0:T(1024)(128)(4,1)} %bitcast.42), calls=%async_computation | async-start | bytes 8388608
  88.0 7.1 %slice-start.1 = ((s8[6291456]{0:T(1024)(128)(4,1)}), s8[2097152]{0:T(1024)(128)(4,1)S(1)}, s32[]{:S(2)}) async-start(s8[6291456]{0:T(1024)(128)(4,1)} %bitcast.42), calls=%async_computation.1 | async-start | bytes 4194304
where the time goes:
time: 178 us; the launch traced here: 176 us
  Pallas kernels  141 us (79%)
  matrix products  18 us (10%)
  other arithmetic  10.6 us (6%)
  local copies, waits for them, and re-layouts  5.49 us (3%)
    pallas_call x2, Pallas kernels, exchange(): pl.pallas_call(functools.partial(exchange_kernel, sizes, total, src_at, d...  67.3 us
    pallas_call x1, Pallas kernels, finish(): pl.pallas_call(functools.partial(finish_kernel, sizes), out_shape=[jax.Sh...  37.3 us
    pallas_call x1, Pallas kernels, spread(): pl.pallas_call(functools.partial(spread_kernel, sizes), out_shape=[jax.Sh...  36.8 us
    dot_general x1, matrix products, attend(): jnp.einsum('nkgd,nkld->nkgl', grouped, cache_keys, preferred_element_type...  6.57 us
    dot_general x1, matrix products, local(): jnp.dot(rows.reshape(total * seqs, q_cols), w_output, preferred_element_t...  6.2 us
    unnamed x12, local copies, waits for them, and re-layouts  3.89 us

commit v1 on v0

--- a/solution.py
+++ b/solution.py
@@ -1,4 +1,5 @@
 import functools
+import math
 
 import jax
 import jax.numpy as jnp
@@ -116,165 +117,384 @@
     )(*arrays)
 
 
-def spread_kernel(
-    sizes, x_ref, ss_ref, all_ref, sums_ref, held, s0, r0, s1, r1, s2, r2, sa, ra, sb, rb, own
+pieces = 4
+lanes = 128
+
+
+def near(sizes):
+    groups, shards = sizes
+    g, s = lax.axis_index("group"), lax.axis_index("shard")
+    out = [(g, lax.rem(s + d, shards)) for d in range(1, shards)]
+    return out + [(lax.rem(g + d, groups), s) for d in range(1, groups)]
+
+
+def meet(sizes):
+    barrier = pltpu.get_barrier_semaphore()
+    partners = near(sizes)
+    for where in partners:
+        pl.semaphore_signal(barrier, inc=1, device_id=device(*where), device_id_type=MESH)
+    pl.semaphore_wait(barrier, len(partners))
+
+
+def turn(j, g, groups):
+    up, down = groups - 1 - g, g
+    both = jnp.minimum(up, down)
+    paired = jnp.where(lax.rem(j, 2) == 0, groups - 1 - j // 2, j // 2)
+    rest = jnp.where(up > down, groups - 1 - (j - both), j - both)
+    return jnp.where(j < 2 * both, paired, jnp.where(j == groups - 1, g, rest))
+
+
+def wait_for(dst, sem):
+    pltpu.make_async_copy(dst, dst, sem).wait()
+
+
+def front_kernel(
+    sizes,
+    x_ref,
+    gain_ref,
+    pos_ref,
+    freq_ref,
+    wq_ref,
+    wkv_ref,
+    got_ref,
+    stage,
+    block,
+    ss,
+    sums,
+    totals,
+    weight,
+    normed,
+    inbuf,
+    outbuf,
+    fin,
+    cosines,
+    sines,
+    load,
+    own,
+    s1,
+    r1,
+    s2,
+    r2,
+    s3,
+    r3,
+    s4,
+    r4,
+    sp,
+    rp,
+    sg,
+    rg,
+    s5,
+    r5,
+    s6,
+    r6,
 ):
     groups, shards = sizes
     chips = shards // 2
-    ratio = shards // groups
-    rows = x_ref.shape[0] // shards
-    width = x_ref.shape[1]
+    span, width = x_ref.shape[1:]
+    tokens = span * chips
+    seqs = tokens // shards
+    depth = weight.shape[0]
+    q_cols = wq_ref.shape[1]
+    blocks, _, _, wide = fin.shape
     g, s = lax.axis_index("group"), lax.axis_index("shard")
     chip, core = s // 2, lax.rem(s, 2)
     sibling = chip * 2 + 1 - core
-    keep = pltpu.make_async_copy(ss_ref, sums_ref.at[g, s], own.at[0])
-    keep.start()
-    greet(sizes, groups * shards)
-    to_group, piece = s // ratio, lax.rem(s, ratio)
-
-    def hop(ds):
-        t = lax.rem(s + ds, shards)
-        src = x_ref.at[pl.ds(pl.multiple_of(t * rows, rows), rows), :]
-        dst = held.at[g, :, pl.ds(pl.multiple_of(piece * width, width), width)]
-        return src, dst, (to_group, t)
-
-    slot = g * ratio + piece
-    for ds in range(1, shards):
-        src, dst, where = hop(ds)
-        remote(src, dst, s0.at[ds], r0.at[slot], where).start()
-    src, dst, where = hop(0)
-
-    @pl.when(to_group != g)
-    def _():
-        remote(src, dst, s0.at[0], r0.at[slot], where).start()
-
-    @pl.when(to_group == g)
-    def _():
-        pltpu.make_async_copy(src, dst, r0.at[slot]).start()
-
-    def plane_sum(ds, sent):
-        to, back = lax.rem(s + ds, shards), lax.rem(s - ds + shards, shards)
-        slot = s if sent else back
-        return remote(ss_ref, sums_ref.at[g, slot], s1.at[ds], r1.at[ds], (g, to))
-
-    def group_sum(dg, sent):
-        to, back = lax.rem(g + dg, groups), lax.rem(g - dg + groups, groups)
-        slot = g if sent else back
-        return remote(sums_ref.at[g], sums_ref.at[slot], s2.at[dg], r2.at[dg], (to, s))
-
-    for ds in range(1, shards):
-        plane_sum(ds, True).start()
-
-    order = sorted(range(groups), key=lambda d: min(d, groups - d))
-
-    def came(dg):
-        return lax.rem(g - dg + groups, groups)
-
-    def ring(dg, c):
+    loads = [
+        pltpu.make_async_copy(wq_ref, weight.at[:, pl.ds(0, q_cols)], load.at[0]),
+        pltpu.make_async_copy(
+            wkv_ref, weight.at[:, pl.ds(q_cols, wkv_ref.shape[1])], load.at[1]
+        ),
+    ]
+    for c in loads:
+        c.start()
+    meet(sizes)
+
+    def half(which):
+        return pl.ds(pl.multiple_of(which * width, width), width)
+
+    def scatter(d):
+        t = lax.rem(chip + d, chips)
+        return remote(x_ref.at[t], stage.at[chip], s1.at[d], r1.at[chip], (g, t * 2 + core))
+
+    for d in range(1, chips):
+        scatter(d).start()
+
+    part = jnp.zeros((tokens, lanes), F32)
+    for j in range(width // lanes):
+        v = x_ref[:, :, j * lanes : (j + 1) * lanes].reshape(tokens, lanes).astype(F32)
+        part = part + v * v
+    ss[...] = jnp.sum(part.T, axis=0, keepdims=True)
+    sums[s] = ss[...]
+
+    def plane_sum(d, slot):
+        return remote(ss, sums.at[slot], sp.at[d], rp.at[d], (g, lax.rem(s + d, shards)))
+
+    for d in range(1, shards):
+        plane_sum(d, s).start()
+
+    def lift(c, src):
+        return remote(src, block.at[g, chip, :, half(core)], s2.at[c], r2.at[g], (c, s))
+
+    def pass_on(j, carry):
+        c = turn(j, g, groups)
+
+        @pl.when(c != chip)
+        def _():
+            wait_for(stage.at[c], r1.at[c])
+
+        @pl.when((c != g) & (c != chip))
+        def _():
+            lift(c, stage.at[c]).start()
+
+        @pl.when((c != g) & (c == chip))
+        def _():
+            lift(c, x_ref.at[c]).start()
+
+        dst = block.at[g, chip, :, half(core)]
+
+        @pl.when((c == g) & (c != chip))
+        def _():
+            pltpu.make_async_copy(stage.at[c], dst, r2.at[g]).start()
+
+        @pl.when((c == g) & (c == chip))
+        def _():
+            pltpu.make_async_copy(x_ref.at[c], dst, r2.at[g]).start()
+
+        return carry
+
+    lax.fori_loop(0, groups, pass_on, 0)
+
+    for d in range(1, shards):
+        plane_sum(d, lax.rem(s - d + shards, shards)).wait_recv()
+    total = sums[0]
+    for t in range(1, shards):
+        total = total + sums[t]
+    totals[g] = total
+
+    def group_sum(d, slot):
+        return remote(
+            totals.at[g], totals.at[slot], sg.at[d], rg.at[d], (lax.rem(g + d, groups), s)
+        )
+
+    for d in range(1, groups):
+        group_sum(d, g).start()
+
+    def ring(p, c):
+        ref = block.at[p, chip, :, half(core)]
         to = lax.rem(chip + c, chips) * 2 + core
-        return remote(
-            held.at[came(dg)], all_ref.at[s, came(dg)], sa.at[dg, c], ra.at[dg, c], (g, to)
+        return remote(ref, ref, s3.at[p, c], r3.at[p, c], (g, to))
+
+    def ring_at(p, c, which):
+        return block.at[p, lax.rem(chip + chips - c, chips), :, half(which)]
+
+    def pair(p, c):
+        ref = ring_at(p, c, core)
+        return remote(ref, ref, s4.at[p, c], r4.at[p, c], (g, sibling))
+
+    def share(j, carry):
+        p = turn(j, g, groups)
+        wait_for(block.at[p, chip, :, half(core)], r2.at[p])
+        for c in range(1, chips):
+            ring(p, c).start()
+        pair(p, 0).start()
+        return carry
+
+    lax.fori_loop(0, groups, share, 0)
+
+    position = jnp.broadcast_to(pos_ref[...].astype(F32), (lanes, tokens)).T
+    angle = position * freq_ref[...]
+    low = lax.broadcasted_iota(jnp.int32, (tokens, lanes), 1) < lanes // 2
+    cosines[...] = jnp.cos(angle)
+    sine = jnp.sin(angle)
+    sines[...] = jnp.where(low, -sine, sine)
+
+    for d in range(1, groups):
+        group_sum(d, lax.rem(g - d + groups, groups)).wait_recv()
+    for c in loads:
+        c.wait()
+
+    def slot_of(p, to, frm):
+        return jnp.where((p == to) & (frm > to), groups, p)
+
+    def send(p, n):
+        to = jnp.where(p > g, g + 1, g - 1)
+        slot = slot_of(p, to, g)
+        return remote(outbuf.at[p, n], inbuf.at[slot, n], s5.at[p, n], r5.at[slot, n], (to, s))
+
+    def product(n):
+        return jnp.dot(
+            normed[...],
+            weight[:, pl.ds(pl.multiple_of(n * wide, wide), wide)],
+            preferred_element_type=F32,
         )
 
-    def pair(dg, c):
-        if c == 0:
-            src, dst = held.at[came(dg)], all_ref.at[s, came(dg)]
-        else:
-            u = lax.rem(chip + chips - c, chips) * 2 + core
-            src = dst = all_ref.at[u, came(dg)]
-        return remote(src, dst, sb.at[dg, c], rb.at[dg, c], (g, sibling))
-
-    def ring_slot(dg, c, which):
-        u = lax.rem(chip + chips - c, chips) * 2 + which
-        return all_ref.at[u, came(dg)]
-
-    def forward(dg):
+    def prepare(p):
         for c in range(1, chips):
-            dst = ring_slot(dg, c, core)
-            remote(dst, dst, sa.at[dg, c], ra.at[dg, c], (g, sibling)).wait_recv()
-            pair(dg, c).start()
-
-    def mine(dg):
-        return pltpu.make_async_copy(
-            held.at[came(dg)], all_ref.at[s, came(dg)], own.at[1 + dg]
-        )
-
-    for i, dg in enumerate(order):
-        for h in range(ratio):
-            dst = held.at[came(dg), :, pl.ds(h * width, width)]
-            pltpu.make_async_copy(dst, dst, r0.at[came(dg) * ratio + h]).wait()
+            wait_for(ring_at(p, c, core), r3.at[p, c])
+            pair(p, c).start()
+        for c in range(chips):
+            wait_for(ring_at(p, c, 1 - core), r4.at[p, c])
+        inverse = lax.rsqrt(totals[p] / (depth * groups) + epsilon)
+        inverse = jnp.broadcast_to(inverse, (lanes, tokens)).T
+        for j in range(depth // lanes):
+            cols = pl.ds(j * lanes, lanes)
+            v = block[p, :, :, cols].reshape(tokens, lanes).astype(F32)
+            normed[:, cols] = (v * inverse * gain_ref[:, cols]).astype(BF)
+
+    def reduce(j, carry):
+        p = turn(j, g, groups)
+        prepare(p)
+        fed = jnp.where(p > g, g > 0, g < groups - 1)
+
+        def columns(n, carry):
+            outbuf[p, n] = product(n).astype(BF)
+
+            @pl.when(fed)
+            def _():
+                wait_for(inbuf.at[p, n], r5.at[p, n])
+                outbuf[p, n] = (outbuf[p, n].astype(F32) + inbuf[p, n].astype(F32)).astype(BF)
+
+            send(p, n).start()
+            return carry
+
+        lax.fori_loop(0, blocks, columns, 0)
+        return carry
+
+    lax.fori_loop(0, groups - 1, reduce, 0)
+    prepare(g)
+    is_key = s < shards // 2
+
+    def deliver(n, d, slot):
+        t = lax.rem(s + d, shards)
+        return remote(fin.at[n, t], got_ref.at[slot, n], s6.at[n, d], r6.at[n, d], (g, t))
+
+    def finish_own(n, carry):
+        acc = product(n)
+        above = jnp.where(g > 0, 1.0, 0.0)
+        below = jnp.where(g < groups - 1, 1.0, 0.0)
+
+        @pl.when(g == 0)
+        def _():
+            inbuf[g, n] = jnp.zeros_like(inbuf[g, n])
+
+        @pl.when(g == groups - 1)
+        def _():
+            inbuf[groups, n] = jnp.zeros_like(inbuf[groups, n])
+
+        @pl.when(g > 0)
+        def _():
+            wait_for(inbuf.at[g, n], r5.at[g, n])
+
+        @pl.when(g < groups - 1)
+        def _():
+            wait_for(inbuf.at[groups, n], r5.at[groups, n])
+
+        acc = acc + inbuf[g, n].astype(F32) + inbuf[groups, n].astype(F32)
+        turned = is_key | (n * wide < q_cols)
+        cosine = jnp.where(turned, cosines[...], 1.0)
+        sine = jnp.where(turned, sines[...], 0.0)
+        for h in range(wide // lanes):
+            v = acc[:, h * lanes : (h + 1) * lanes]
+            v = v * cosine + pltpu.roll(v, lanes // 2, 1) * sine
+            fin[n, :, :, pl.ds(h * lanes, lanes)] = v.reshape(shards, seqs, lanes).astype(BF)
+        got_ref[s, n] = fin[n, s]
+        for d in range(1, shards):
+            deliver(n, d, s).start()
+        return carry
+
+    lax.fori_loop(0, blocks, finish_own, 0)
+
+    def settle(n, carry):
+        for d in range(1, shards):
+            deliver(n, d, lax.rem(s - d + shards, shards)).wait()
+        return carry
+
+    lax.fori_loop(0, blocks, settle, 0)
+
+    def drain(j, carry):
+        p = turn(j, g, groups)
+
+        def each(n, carry):
+            send(p, n).wait_send()
+            return carry
+
+        lax.fori_loop(0, blocks, each, 0)
+        return carry
+
+    lax.fori_loop(0, groups - 1, drain, 0)
+    for d in range(1, chips):
+        scatter(d).wait_send()
+    for d in range(1, shards):
+        plane_sum(d, s).wait_send()
+    for d in range(1, groups):
+        group_sum(d, g).wait_send()
+
+    def drain_block(p, carry):
+        @pl.when(p != g)
+        def _():
+            lift(p, x_ref.at[p]).wait_send()
+
+        pair(p, 0).wait_send()
         for c in range(1, chips):
-            ring(dg, c).start()
-        pair(dg, 0).start()
-        mine(dg).start()
-        if i == 0:
-            keep.wait()
-            for ds in range(1, shards):
-                plane_sum(ds, False).wait_recv()
-            for d in range(1, groups):
-                group_sum(d, True).start()
-        else:
-            forward(order[i - 1])
-    forward(order[-1])
-    for dg in order:
-        for c in range(chips):
-            dst = ring_slot(dg, c, 1 - core)
-            remote(dst, dst, sb.at[dg, c], rb.at[dg, c], (g, sibling)).wait_recv()
-    for dg in order:
-        for c in range(chips):
-            if c:
-                ring(dg, c).wait_send()
-            pair(dg, c).wait_send()
-        mine(dg).wait()
-    for ds in range(1, shards):
-        src, dst, where = hop(ds)
-        remote(src, dst, s0.at[ds], r0.at[slot], where).wait_send()
-        plane_sum(ds, True).wait_send()
-    src, dst, where = hop(0)
-
-    @pl.when(to_group != g)
-    def _():
-        remote(src, dst, s0.at[0], r0.at[slot], where).wait_send()
-
-    for d in range(1, groups):
-        group_sum(d, True).wait_send()
-        group_sum(d, False).wait_recv()
-
-
-def spread(x, ss, sizes):
+            ring(p, c).wait_send()
+            pair(p, c).wait_send()
+        return carry
+
+    lax.fori_loop(0, groups, drain_block, 0)
+
+
+def front(x, gain, positions, frequencies, w_query, w_keyval, sizes):
     groups, shards = sizes
-    ratio = shards // groups
-    rows = x.shape[0] // shards
-    wide = x.shape[1] * ratio
+    chips = shards // 2
+    tokens, width = x.shape
+    span = tokens // chips
+    seqs = tokens // shards
+    depth = w_query.shape[0]
+    cols = w_query.shape[1] + w_keyval.shape[1]
+    wide = math.gcd(cols, 256)
+    wide = math.gcd(wide, w_query.shape[1])
+    blocks = cols // wide
     dma = pltpu.SemaphoreType.DMA
+    hbm = pl.BlockSpec(memory_space=pl.ANY)
     return pl.pallas_call(
-        functools.partial(spread_kernel, sizes),
-        out_shape=[
-            jax.ShapeDtypeStruct((shards, groups, rows, wide), x.dtype),
-            jax.ShapeDtypeStruct((groups, shards) + ss.shape, ss.dtype),
-        ],
-        in_specs=[VMEM] * 2,
-        out_specs=[VMEM] * 2,
+        functools.partial(front_kernel, sizes),
+        out_shape=jax.ShapeDtypeStruct((shards, blocks, seqs, wide), BF),
+        in_specs=[VMEM] * 4 + [hbm] * 2,
+        out_specs=VMEM,
         scratch_shapes=[
-            pltpu.VMEM((groups, rows, wide), x.dtype),
-            dma((shards,)),
-            dma((shards,)),
+            pltpu.VMEM((chips, span, width), BF),
+            pltpu.VMEM((groups, chips, span, depth), BF),
+            pltpu.VMEM((1, tokens), F32),
+            pltpu.VMEM((shards, 1, tokens), F32),
+            pltpu.VMEM((groups, 1, tokens), F32),
+            pltpu.VMEM((depth, cols), BF),
+            pltpu.VMEM((tokens, depth), BF),
+            pltpu.VMEM((groups + 1, blocks, tokens, wide), BF),
+            pltpu.VMEM((groups, blocks, tokens, wide), BF),
+            pltpu.VMEM((blocks, shards, seqs, wide), BF),
+            pltpu.VMEM((tokens, lanes), F32),
+            pltpu.VMEM((tokens, lanes), F32),
+            dma((2,)),
+            dma((1,)),
+            dma((chips,)),
+            dma((chips,)),
+            dma((groups,)),
+            dma((groups,)),
+            dma((groups, chips)),
+            dma((groups, chips)),
+            dma((groups, chips)),
+            dma((groups, chips)),
             dma((shards,)),
             dma((shards,)),
             dma((groups,)),
             dma((groups,)),
-            dma((groups, shards // 2)),
-            dma((groups, shards // 2)),
-            dma((groups, shards // 2)),
-            dma((groups, shards // 2)),
-            dma((1 + groups,)),
+            dma((groups, blocks)),
+            dma((groups + 1, blocks)),
+            dma((blocks, shards)),
+            dma((blocks, shards)),
         ],
         compiler_params=pltpu.CompilerParams(collective_id=1, has_side_effects=True),
-    )(x, ss)
-
-
-pieces = 4
-lanes = 128
+    )(x.reshape(chips, span, width), gain, positions, frequencies, w_query, w_keyval)
 
 
 def finish_kernel(
@@ -445,24 +665,6 @@
     )(partial, x, gain)
 
 
-def rotate(heads_block, position):
-    head_dim = heads_block.shape[-1]
-    half_dim = head_dim // 2
-    frequency = rope_base ** (-2.0 * jnp.arange(half_dim, dtype=jnp.float32) / head_dim)
-    angles = position.astype(jnp.float32)[:, None] * frequency[None, :]
-    cosine = jnp.cos(angles)[:, None, :]
-    sine_part = jnp.sin(angles)[:, None, :]
-    lower_half = heads_block[..., :half_dim]
-    upper_half = heads_block[..., half_dim:]
-    return jnp.concatenate(
-        [
-            lower_half * cosine - upper_half * sine_part,
-            upper_half * cosine + lower_half * sine_part,
-        ],
-        axis=-1,
-    )
-
-
 def attend(grouped, new_keys, new_values, cache_keys, cache_values, lengths):
     cache_len, head_dim = cache_keys.shape[2:]
     score_scale = head_dim ** (-0.5)
@@ -512,42 +714,17 @@
     model = width * shards
     depth = w_query.shape[0]
     q_cols, kv_cols = w_query.shape[1], w_keyval.shape[1]
-    resident = hidden_state.astype(F32)
-
-    squares = jnp.sum(resident * resident, axis=1)[None, :]
-    block, sums = spread(hidden_state, squares, sizes)
-    square_sum = jnp.sum(sums[:, :, 0, :], axis=1)
-    inverse = lax.rsqrt(square_sum / model + epsilon)
-    inverse = inverse.reshape(groups, shards, seqs).transpose(1, 0, 2)
-    gain = lax.dynamic_slice_in_dim(attn_gain, g * depth, depth).astype(F32)
-    normed = (block.astype(F32) * inverse[..., None] * gain).astype(BF)
-    normed = normed.reshape(total * seqs, depth)
-    part_q = jnp.dot(normed, w_query, preferred_element_type=F32).astype(BF)
-    part_kv = jnp.dot(normed, w_keyval, preferred_element_type=F32).astype(BF)
-    cols = q_cols + kv_cols
-    part = jnp.concatenate([part_q, part_kv], axis=1)
-
-    (got,) = exchange(
-        [part.reshape(shards, groups, seqs, cols)],
-        [(groups, shards, seqs, cols)],
-        sizes,
-        total,
-        lambda ref, pg, ps: ref.at[ps, pg],
-        lambda ref, pg, ps: ref.at[pg, ps],
-        2,
-    )
+    gain = lax.dynamic_slice_in_dim(attn_gain, g * depth, depth).astype(F32)[None, :]
+    half_dim = head_dim // 2
+    frequency = rope_base ** (-2.0 * jnp.arange(half_dim, dtype=F32) / head_dim)
+    frequency = jnp.concatenate([frequency, frequency])[None, :]
+    got = front(hidden_state, gain, lengths[None, :], frequency, w_query, w_keyval, sizes)
     owner_len = lax.dynamic_slice_in_dim(lengths, s * seqs, seqs)
-    fresh = jnp.sum(got.astype(F32), axis=0).transpose(1, 0, 2)
-    queries, keyval = fresh[..., :q_cols], fresh[..., q_cols:]
     heads = shards * q_cols // head_dim
-    grouped = (
-        rotate(queries.reshape(seqs, heads, head_dim), owner_len)
-        .astype(BF)
-        .reshape(seqs, kv_heads, heads // kv_heads, head_dim)
-    )
-    keyval = keyval.reshape(seqs, 2 * kv_heads, head_dim)
-    new_keys = rotate(keyval[:, :kv_heads], owner_len).astype(BF)
-    new_values = keyval[:, kv_heads:].astype(BF)
+    fresh = got.transpose(2, 0, 1, 3).reshape(seqs, shards, q_cols + kv_cols)
+    grouped = fresh[..., :q_cols].reshape(seqs, kv_heads, heads // kv_heads, head_dim)
+    keyval = fresh[..., q_cols:].reshape(seqs, 2 * kv_heads, head_dim)
+    new_keys, new_values = keyval[:, :kv_heads], keyval[:, kv_heads:]
     context = attend(grouped, new_keys, new_values, cache_keys, cache_values, owner_len)
     context = context.reshape(seqs, shards, q_cols).transpose(1, 0, 2)
 

time: 178 us -> 158 us (0.89)
  Pallas kernels: 141 us -> 129 us
  other arithmetic: 10.6 us -> 3.7 us
    pallas_call x2 -> x1, Pallas kernels: 67.3 us -> 34.7 us  [exchange(): pl.pallas_call(functools.partial(exchange_kernel, sizes, total, src_at, d...]
    pallas_call x1, Pallas kernels: 36.8 us -> 56.3 us  [front(): pl.pallas_call(functools.partial(front_kernel, sizes), out_shape=jax.Shap...]
    reduce_sum x3 -> x0, other arithmetic: 3.9 us -> none  [the longest x1 1.59 us: local(): squares = jnp.sum(resident * resident, axis=1)[None, :]]
    convert_element_type x3 -> x0, other arithmetic: 3.14 us -> none  [the longest x1 2.28 us: local(): normed = (block.astype(F32) * inverse[..., None] * gain).astype(BF)]
    dot_general x2 -> x0, matrix products: 3.05 us -> none  [the longest x1 2.34 us: local(): part_q = jnp.dot(normed, w_query, preferred_element_type=F32).astype(BF)]
    dot_general x1, matrix products: 1.84 us -> 4.63 us  [attend(): jnp.einsum('nkgl,nkld->nkgd', weight_bf, cache_values, preferred_element_...]
    broadcast_in_dim x0 -> x2, other arithmetic: none -> 1.88 us  [the longest x1 1.29 us: local(): lax.dynamic_slice_in_dim(attn_gain, g * depth, depth).astype(F32)[None, :]]
    unnamed x12 -> x3, local copies, waits for them, and re-layouts: 3.89 us -> 3.36 us
where the time goes in v1:
time: 158 us; the launch traced here: 157 us
  Pallas kernels  129 us (82%)
  matrix products  17.3 us (11%)
  local copies, waits for them, and re-layouts  6.19 us (4%)
  other arithmetic  3.7 us (2%)
    pallas_call x1, Pallas kernels, front(): pl.pallas_call(functools.partial(front_kernel, sizes), out_shape=jax.Shap...  56.3 us
    pallas_call x1, Pallas kernels, finish(): pl.pallas_call(functools.partial(finish_kernel, sizes), out_shape=[jax.Sh...  37.7 us
    pallas_call x1, Pallas kernels, exchange(): pl.pallas_call(functools.partial(exchange_kernel, sizes, total, src_at, d...  34.7 us
    dot_general x1, matrix products, local(): jnp.dot(rows.reshape(total * seqs, q_cols), w_output, preferred_element_t...  6.2 us
    dot_general x1, matrix products, attend(): jnp.einsum('nkgd,nkld->nkgl', grouped, cache_keys, preferred_element_type...  6.2 us
    dot_general x1, matrix products, attend(): jnp.einsum('nkgl,nkld->nkgd', weight_bf, cache_values, preferred_element_...  4.63 us
    unnamed x3, local copies, waits for them, and re-layouts  3.36 us

profile of v1, /device:TPU:0, one launch (start us, length us, event | category | flops | bytes accessed | tf_op | source)
XLA Modules:
  0.0 156.6 jit_solution(15196385667330082224)
XLA Ops:
  0.6 0.7 dynamic_slice.9
  1.4 0.1 iota_compare_fusion
  1.4 1.3 dynamic-slice_convert_fusion
  2.7 0.6 maximum_bitcast_fusion.freq_ref
  3.3 56.3 %shard_map.104 = bf16[8,5,16,256]{3,2,1,0:T(8,128)(2,1)} custom-call(bf16[4,32,1024]{2,1,0:T(8,128)(2,1)} %bitcast.38, f32[1,2048]{1,0:T(1,128)} %bitcast.43, s32[1,128]{1,0:T(1,128)} %bitcast.45, f32[1,128]{1,0:T(1,128)} %maximum_bitcast_fusion.freq_ref, bf16[2048,1024]{1,0:T(8,128)(2,1)} %wq_ref.1, bf16[2048,256]{1,0:T(8,128)(2,1)} %wkv_ref.1), custom_call_target="tpu_custom_call" | custom-call | tf_op jit(solution)/shard_map/pallas_call | solution.py:459
  59.7 1.1 copy.12
  60.8 6.2 %fusion.13 = (f32[16,8,8]{2,1,0:T(8,128)S(1)}, f32[16,8,8,192]{3,2,1,0:T(8,128)S(1)}) fusion(bf16[16,8,192,128]{3,2,1,0:T(8,128)(2,1)} %param.15, bf16[16,8,8,128]{3,1,2,0:T(8,128)(2,1)S(1)} %slice_bitcast_fusion, pred[16,192]{1,0:T(8,128)(4,1)S(1)} %iota_compare_fusion), kind=kOutput, calls=%fused_computation.30 | convolution fusion | flops 50920448 | bytes 7347200 | tf_op jit(solution)/shard_map/nkgd,nkld->nkgl/dot_general | solution.py:672
  67.0 0.1 reshape.49
  67.1 0.3 fusion.5
  67.4 0.4 fusion.2
  67.8 4.6 %fusion.1 = bf16[16,8,8,128]{3,2,1,0:T(8,128)(2,1)S(1)} fusion(bf16[16,8,192,128]{3,2,1,0:T(8,128)(2,1)} %param.16, f32[16,8,8,192]{3,2,1,0:T(8,128)S(1)} %get-tuple-element.7, f32[16,8,8]{2,1,0:T(8,128)S(1)} %get-tuple-element.3, f32[16,8,8]{2,1,0:T(8,128)S(1)} %multiply_maximum_fusion, f32[16,8,128]{2,1,0:T(8,128)S(1)} %get-tuple-element.4, ...), kind=kOutput, calls=%fused_computation.4 | convolution fusion | flops 51314688 | bytes 7417856 | tf_op jit(solution)/shard_map/nkgl,nkld->nkgd/dot_general | solution.py:687
  72.4 0.1 reshape.57
  72.6 0.9 copy.31
  73.4 34.7 %shard_map.105 = bf16[4,8,16,1024]{3,2,1,0:T(8,128)(2,1)} custom-call(bf16[8,16,1024]{2,1,0:T(8,128)(2,1)} %bitcast.40), custom_call_target="tpu_custom_call" | custom-call | tf_op jit(solution)/shard_map/pallas_call | solution.py:106
  108.1 6.2 %convolution_convert_fusion = bf16[512,2048]{1,0:T(8,128)(2,1)} fusion(bf16[512,1024]{1,0:T(8,128)(2,1)} %bitcast.39, bf16[1024,2048]{1,0:T(8,128)(2,1)} %param.14), kind=kOutput, calls=%fused_computation | convolution fusion | flops 2148532224 | bytes 7340032 | tf_op jit(solution)/shard_map/dot_general | solution.py:740
  114.3 1.3 dynamic-slice_convert_fusion.1
  115.6 37.7 %shard_map.106 = (bf16[128,1024]{1,0:T(8,128)(2,1)}, bf16[128,1024]{1,0:T(8,128)(2,1)}) custom-call(bf16[4,128,2048]{2,1,0:T(8,128)(2,1)} %bitcast.34, bf16[128,1024]{1,0:T(8,128)(2,1)} %x_ref.1, f32[1,1024]{1,0:T(1,128)} %bitcast.44), custom_call_target="tpu_custom_call" | custom-call | tf_op jit(solution)/shard_map/pallas_call | solution.py:643
  153.3 1.7 %copy.34 = bf16[128,1024]{1,0:T(8,128)(2,1)} copy(bf16[128,1024]{1,0:T(8,128)(2,1)} %get-tuple-element.10) | data formatting | bytes 524288
  155.0 1.7 %copy.35 = bf16[128,1024]{1,0:T(8,128)(2,1)} copy(bf16[128,1024]{1,0:T(8,128)(2,1)} %get-tuple-element.11) | data formatting | bytes 524288
  (6 shorter events, 0.1 us)
